TPU v7x, 32 devices: a whole 2x2x4 slice. The times are simulated.
32 devices in a mesh: row: 8 (over y, x, core), col: 4 (over z).
Axes of the slice: x: 2, y: 2, z: 4, core: 2. Of those that a mesh axis runs over, the one named last changes fastest.
Arguments:
- integrals: bfloat16 [320, 32, 4096], P('row', None, 'col'), may hold values from -6 to 6
- coeffs: bfloat16 [10240, 4096], P('row', 'col'), may hold values from -0.078125 to 0.078125
- mask: int32 [320, 4], replicated, may hold values from 0 to 1, as said below
- offsets: int32 [321], replicated, may hold values from 0 to 7680, as said below
- atom_of_slot: int32 [320], replicated, may hold values from 0 to 319, as said below
Outputs:
- half_transformed: bfloat16 [4096, 4096], P('row', 'col')
Inputs may be any that keep to these rules, and one draw needn't show every extreme that they name: `mask`: 1 marks a significant pair of an atom and a block of 64 window functions. offsets[0] = 0 and offsets[a + 1] - offsets[a] is atom a's number of basis functions, 16 to 32; atoms 2k and 2k + 1 together have 3 * 16; rows of an atom's padded block past its number are padding. `atom_of_slot`: a permutation of the atoms; slot k is held by atom owner k // 40 along row, and atom a's AO-row owner is a // 40; one atom owner holds at least one and at most 5 atoms of any one AO-row owner, and exactly 5 for some pairs.
All inputs are finite; a program needn't handle non-finite values.
Results may differ from a plain program's by a relative error of at most 0.015.
Values may be sent and summed in bfloat16 or wider, within the bound.
A program may use at most 256 MiB of HBM per device.

v0:
```python
import jax
import jax.numpy as jnp
from jax import lax
from jax.sharding import PartitionSpec as P


def body(integrals, coeffs, mask, offsets, atom_of_slot):
    n_row = lax.axis_size("row")
    own_row = lax.axis_index("row")
    own_col = lax.axis_index("col")
    per_dev, atom_w, row_width = integrals.shape
    slots_cap = max(2, -(-per_dev // n_row))
    counter = jnp.arange(per_dev, dtype=jnp.int32)
    slot_count = n_row * slots_cap
    mine_slots = lax.dynamic_slice_in_dim(atom_of_slot, own_row * per_dev, per_dev)
    target = mine_slots // per_dev
    before = (target[None, :] == target[:, None]) & (counter[None, :] < counter[:, None])
    arrival_rank = jnp.sum(before.astype(jnp.int32), axis=1)
    position = target * slots_cap + arrival_rank
    placing = (jnp.arange(slot_count, dtype=jnp.int32)[:, None] == position[None, :]).astype(
        jnp.bfloat16
    )
    outgoing = jnp.dot(
        placing, integrals.reshape(per_dev, atom_w * row_width), preferred_element_type=jnp.bfloat16
    )
    outgoing = outgoing.reshape(n_row, slots_cap, atom_w * row_width)
    incoming = lax.all_to_all(outgoing, "row", split_axis=0, concat_axis=0, tiled=True)
    holders = atom_of_slot.reshape(n_row, per_dev)
    is_mine = holders // per_dev == own_row
    arrival = jnp.cumsum(is_mine.astype(jnp.int32), axis=1) - 1
    slot_of = jnp.arange(n_row, dtype=jnp.int32)[:, None] * slots_cap + arrival
    local_atom = holders - own_row * per_dev
    pick_atom = (
        (local_atom.reshape(-1)[:, None] == counter[None, :]) & is_mine.reshape(-1)[:, None]
    ).astype(jnp.float32)
    pick_slot = (
        slot_of.reshape(-1)[:, None] == jnp.arange(slot_count, dtype=jnp.int32)[None, :]
    ).astype(jnp.float32)
    gather_matrix = jnp.dot(pick_atom.T, pick_slot).astype(jnp.bfloat16)
    ordered = jnp.dot(
        gather_matrix,
        incoming.reshape(slot_count, atom_w * row_width),
        preferred_element_type=jnp.bfloat16,
    )
    ordered = ordered.reshape(per_dev, atom_w, row_width)
    bounds = lax.dynamic_slice_in_dim(offsets, own_row * per_dev, per_dev + 1)
    lengths = bounds[1:] - bounds[:-1]
    significant = lax.dynamic_slice(mask, (own_row * per_dev, own_col), (per_dev, 1))[:, 0] > 0
    keep_rows = (jnp.arange(atom_w, dtype=jnp.int32)[None, :] < lengths[:, None]) & significant[
        :, None
    ]
    blocks = ordered * keep_rows[:, :, None].astype(jnp.bfloat16)
    bucket_edges = [0, per_dev]
    kept_rows = blocks.reshape(per_dev * atom_w, row_width)
    coeff_piece = lax.all_gather(coeffs, "col", axis=1, tiled=True)
    low_row = bucket_edges[0] * atom_w
    high_row = bucket_edges[1] * atom_w

    def product(low_row=low_row, high_row=high_row):
        return lax.dot_general(
            coeff_piece, kept_rows, (((0,), (0,)), ((), ())), preferred_element_type=jnp.float32
        )

    bucket_term = product()
    partial_sums = bucket_term.astype(jnp.bfloat16)
    result = lax.psum_scatter(partial_sums, "row", scatter_dimension=0, tiled=True).astype(
        jnp.float32
    )
    return result.astype(jnp.bfloat16)


def solution(mesh):
    in_specs = (P("row", None, "col"), P("row", "col"), P(), P(), P())
    out_specs = P("row", "col")
    return jax.shard_map(body, mesh=mesh, in_specs=in_specs, out_specs=out_specs, check_vma=False)
```

profile of v0, /device:TPU:7, one launch (start us, length us, event | category | flops | bytes accessed | tf_op | source)
XLA Modules:
  0.0 288.9 jit_solution(10588621491693638440)
XLA Ops:
  6.5 0.7 all-gather.2.cloned.1.call-update
  7.3 3.9 %reshape.121 = bf16[40,32768,1]{1,0,2:T(8,128)(2,1)S(1)} reshape(bf16[40,32,1024]{2,1,0:T(8,128)(2,1)} %param.5) | data formatting | bytes 5242880 | tf_op jit(solution)/shard_map/reshape | solution.py:24
  11.2 0.1 and_select_fusion
  11.3 0.2 convert_reduce_fusion
  11.4 0.1 multiply_add_fusion.1
  11.5 0.1 broadcast_compare_fusion
  11.6 2.9 fusion.16
  14.5 4.6 %all-to-all-start = ((bf16[8,5,32768]{2,1,0:T(8,128)(2,1)}), bf16[8,5,32768]{2,1,0:T(8,128)(2,1)}, u32[]{:S(2)}, u32[]{:S(2)}) async-start(bf16[8,5,32768]{2,1,0:T(8,128)(2,1)} %fusion.16), calls=%async_computation | async-start | bytes 8388608 | tf_op jit(solution)/shard_map/all_to_all | solution.py:27
  19.1 0.1 and.41
  19.2 0.1 div.18
  19.3 0.2 reduce_window_sum.11
  19.5 0.1 add_add_fusion
  19.6 0.1 add.46
  19.7 0.8 dynamic_slice.10
  20.4 0.8 compare_bitcast_fusion
  21.2 0.1 slice_subtract_fusion
  21.3 44.2 %all-to-all-done = bf16[8,5,32768]{2,1,0:T(8,128)(2,1)} async-done(((bf16[8,5,32768]{2,1,0:T(8,128)(2,1)}), bf16[8,5,32768]{2,1,0:T(8,128)(2,1)}, u32[]{:S(2)}, u32[]{:S(2)}) %all-to-all-start) | async-done | bytes 2621472 | tf_op jit(solution)/shard_map/all_to_all | solution.py:27
  65.5 3.4 %reshape.119 = bf16[40,32768]{1,0:T(8,128)(2,1)S(1)} reshape(bf16[8,5,32768]{2,1,0:T(8,128)(2,1)} %all-to-all-done) | data formatting | bytes 5242880 | tf_op jit(solution)/shard_map/reshape | solution.py:42
  68.9 2.7 fusion.3
  71.6 3.2 %copy.17 = bf16[40,32,1024]{2,1,0:T(8,128)(2,1)S(1)} copy(bf16[40,32,1024]{2,0,1:T(8,128)(2,1)} %fusion.3) | data formatting | bytes 5242880 | tf_op jit(solution)/shard_map/mul | solution.py:52
  74.8 119.4 %all-gather.2.cloned.1.call-done = bf16[1280,4096]{1,0:T(8,128)(2,1)} async-done(((bf16[1280,1024]{1,0:T(8,128)(2,1)}), bf16[1280,4096]{1,0:T(8,128)(2,1)}) %all-gather.2.cloned.1.call-update) | async-done | bytes 10485776 | tf_op jit(solution)/shard_map/all_gather | solution.py:55
  194.2 17.2 %convert_bitcast_fusion = bf16[4096,1024]{0,1:T(8,128)(2,1)} fusion(bf16[1280,1024]{1,0:T(8,128)(2,1)S(1)} %bitcast.20, bf16[1280,4096]{1,0:T(8,128)(2,1)} %all-gather.2.cloned.1.call-done), kind=kOutput, calls=%fused_computation | convolution fusion | flops 10741612544 | bytes 21495808 | tf_op jit(solution)/shard_map/dot_general | solution.py:60
  211.4 68.4 %reduce-scatter.2.cloned.1.call-done = bf16[512,1024]{0,1:T(8,128)(2,1)} async-done(((bf16[4096,1024]{0,1:T(8,128)(2,1)}), bf16[512,1024]{0,1:T(8,128)(2,1)}) %reduce-scatter.2.cloned.1.call-update) | async-done | bytes 1048592 | tf_op jit(solution)/shard_map/reduce_scatter | solution.py:66
  279.8 2.3 copy.18
  (11 shorter events, 0.1 us)
Async XLA Ops:
  6.5 187.6 %all-gather.2.cloned.1.call-start = ((), (), s32[]{:S(2)}) async-start(), calls=%async_computation.2 | async-start | bytes 13107200 | tf_op jit(solution)/shard_map/all_gather | solution.py:55
  7.3 3.9 %copy-start = (s32[320]{0:T(512)S(1)}, s32[320]{0:T(512)}, u32[]{:S(2)}) copy-start(s32[320]{0:T(512)} %param.9) | copy-start | bytes 3844
  14.5 51.0 %all-to-all-start = ((bf16[8,5,32768]{2,1,0:T(8,128)(2,1)}), bf16[8,5,32768]{2,1,0:T(8,128)(2,1)}, u32[]{:S(2)}, u32[]{:S(2)}) async-start(bf16[8,5,32768]{2,1,0:T(8,128)(2,1)} %fusion.16), calls=%async_computation | async-start | bytes 8388608 | tf_op jit(solution)/shard_map/all_to_all | solution.py:27
  19.0 260.8 %reduce-scatter.2.cloned.1.call-start = ((), (), s32[]{:S(2)}) async-start(), calls=%async_computation.3 | async-start | bytes 9437184 | tf_op jit(solution)/shard_map/reduce_scatter | solution.py:66
Sparse Core Ops, SparseCore 0:
  8.9 185.2 all-gather.1
  211.5 68.2 reduce-scatter.1
where the time goes:
time: 292 us; the launch traced here: 289 us
  waiting for transfers between devices  233 us (80%)
  matrix products  22.8 us (8%)
  local copies, waits for them, and re-layouts  13.7 us (5%)
  between operations  13.5 us (5%)
  starting transfers between devices  4.6 us (2%)
    all_gather x1, waiting for transfers between devices, body(): coeff_piece = lax.all_gather(coeffs, 'col', axis=1, tiled=True)  119 us
    reduce_scatter x1, waiting for transfers between devices, body(): lax.psum_scatter(partial_sums, 'row', scatter_dimension=0, tiled=True)  68.4 us
    all_to_all x1, waiting for transfers between devices, body(): lax.all_to_all(outgoing, 'row', split_axis=0, concat_axis=0, tiled=True)  44.2 us
    dot_general x1, matrix products, product(): lax.dot_general(coeff_piece, kept_rows, (((0,), (0,)), ((), ())), preferr...  17.2 us
  transfers between devices with their start and end apart: 3, of which 3 were waited for; matrix products, arithmetic and copies ran while one was open for 6% of the time, Pallas kernels for 0%

commit v1 on v0

v1 whole, which is shorter than its diff:
```python
import functools

import jax
import jax.numpy as jnp
from jax import lax
from jax.experimental import pallas as pl
from jax.experimental.pallas import tpu as pltpu
from jax.sharding import PartitionSpec as P

MESH = pl.DeviceIdType.MESH
F32 = jnp.float32
BF16 = jnp.bfloat16


def remote(src, dst, send, recv, device):
    return pltpu.make_async_remote_copy(
        src_ref=src, dst_ref=dst, send_sem=send, recv_sem=recv, device_id=device, device_id_type=MESH
    )


def nearest(me, n, s):
    m = jnp.minimum(me, n - 1 - me)
    step = (s + 1) // 2
    near = jnp.where(s % 2 == 1, me - step, me + step)
    far = jnp.where(me <= n - 1 - me, s, n - 1 - s)
    return jnp.where(s <= 2 * m, near, far)


def kernel(
    n_row, n_col, cap, chunks, width,
    meta, integrals, coeffs, out,
    asend, arecv, kept, gathered, mine1, send1, recv1, sums,
    a_ss, a_rs, r_ss, l_ss, g_rs, s1_ss, s1_rs, s2_ss, s2_rs,
):
    me = lax.axis_index("row")
    plane = lax.axis_index("col")
    core = me % 2
    chip = me // 2
    n_chip = n_row // 2
    partner = me + 1 - 2 * core
    per_dev, atom_w, row_width = integrals.shape
    half = atom_w // 2
    pairs = per_dev // 2
    packed = 3 * half
    slots = n_row * cap
    per_plane = n_row // n_col
    chips_plane = per_plane // 2
    block = width * chunks
    pick0, len0, sig0 = slots, slots + per_dev, slots + 2 * per_dev
    has_left = plane > 0
    has_right = plane < n_col - 1

    barrier = pltpu.get_barrier_semaphore()
    for other in range(1, n_row):
        pl.semaphore_signal(barrier, inc=1, device_id=((me + other) % n_row, plane), device_id_type=MESH)

    @pl.when(has_left)
    def _():
        pl.semaphore_signal(barrier, inc=1, device_id=(me, plane - 1), device_id_type=MESH)

    @pl.when(has_right)
    def _():
        pl.semaphore_signal(barrier, inc=1, device_id=(me, plane + 1), device_id_type=MESH)

    def selection(p, weighted):
        s = lax.broadcasted_iota(jnp.int32, (packed, 2 * atom_w), 0)
        t = lax.broadcasted_iota(jnp.int32, (packed, 2 * atom_w), 1)
        extra = meta[len0 + 2 * p] - half
        source = jnp.where(
            s < half, s, jnp.where(s < 2 * half, s + half, jnp.where(s - 2 * half < extra, s - half, s + half - extra))
        )
        hit = source == t
        if weighted:
            sig = jnp.where(t < atom_w, meta[sig0 + 2 * p], meta[sig0 + 2 * p + 1])
            hit = hit & (sig > 0)
        return jnp.where(hit, 1.0, 0.0).astype(BF16)

    def pack_coeffs(p, carry):
        rows = coeffs[pl.ds(pl.multiple_of(p * 2 * atom_w, 2 * atom_w), 2 * atom_w), :]
        live = jnp.dot(selection(p, False), rows, preferred_element_type=F32).astype(BF16)
        at = pl.ds(pl.multiple_of(p * packed, 16), packed)
        for k in range(chunks):
            for b in range(per_plane):
                lo = b * block + k * width
                gathered[plane, k, at, b * width : (b + 1) * width] = live[:, lo : lo + width]
        return carry

    lax.fori_loop(0, pairs, pack_coeffs, 0)
    pl.semaphore_wait(barrier, n_row - 1 + has_left.astype(jnp.int32) + has_right.astype(jnp.int32))

    def to_right(z, k):
        return remote(gathered.at[z, k], gathered.at[z, k], r_ss.at[z, k], g_rs.at[z, k], (me, plane + 1))

    def to_left(z, k):
        return remote(gathered.at[z, k], gathered.at[z, k], l_ss.at[z, k], g_rs.at[z, k], (me, plane - 1))

    def forward(z, k):
        @pl.when((z <= plane) & has_right)
        def _():
            to_right(z, k).start()

        @pl.when((z >= plane) & has_left)
        def _():
            to_left(z, k).start()

    for k in range(chunks):
        forward(plane, k)

    def a_copy(owner):
        return remote(asend.at[owner], arecv.at[me], a_ss.at[owner], a_rs.at[me], (owner, plane))

    def place(step, carry):
        owner = (me + step) % n_row

        @pl.when(step > 0)
        def _():
            for c in range(cap):
                asend[owner, c] = integrals[meta[owner * cap + c]]
            a_copy(owner).start()

        @pl.when(step == 0)
        def _():
            for c in range(cap):
                arecv[me, c] = integrals[meta[me * cap + c]]

        return carry

    lax.fori_loop(0, n_row, place, 0)

    def wait_blocks(step, carry):
        source = (me + step) % n_row
        remote(asend.at[source], arecv.at[source], a_ss.at[source], a_rs.at[source], (source, plane)).wait_recv()
        return carry

    lax.fori_loop(1, n_row, wait_blocks, 0)

    def pack_kept(p, carry):
        first, second = meta[pick0 + 2 * p], meta[pick0 + 2 * p + 1]
        rows = jnp.concatenate([arecv[first // cap, first % cap], arecv[second // cap, second % cap]], axis=0)
        live = jnp.dot(selection(p, True), rows, preferred_element_type=F32).astype(BF16)
        kept[pl.ds(pl.multiple_of(p * packed, 16), packed), :] = live
        return carry

    lax.fori_loop(0, pairs, pack_kept, 0)

    def core_copy(z, k):
        return remote(send1.at[z, k], recv1.at[z, k], s1_ss.at[z, k], s1_rs.at[z, k], (partner, plane))

    def chip_copy(target, k):
        return remote(
            mine1.at[target, k], sums.at[chip, k], s2_ss.at[target, k], s2_rs.at[chip, k], (2 * target + core, plane)
        )

    total = n_col * chunks

    def step_body(n, carry):
        @pl.when(n < total)
        def _():
            z = nearest(plane, n_col, n // chunks)
            k = n % chunks

            @pl.when(z != plane)
            def _():
                to_right(z, k).wait_recv()
                forward(z, k)

            part = lax.dot_general(
                gathered[z, k], kept[...], (((0,), (0,)), ((), ())), preferred_element_type=F32
            ).astype(BF16)
            for j in range(chips_plane):
                lower = part[2 * j * width : (2 * j + 1) * width]
                upper = part[(2 * j + 1) * width : (2 * j + 2) * width]
                is_lower = core == 0
                mine1[z * chips_plane + j, k] = jnp.where(is_lower, lower, upper)
                send1[z, k, j] = jnp.where(is_lower, upper, lower)
            core_copy(z, k).start()

        @pl.when(n > 0)
        def _():
            z = nearest(plane, n_col, (n - 1) // chunks)
            k = (n - 1) % chunks
            core_copy(z, k).wait_recv()
            for j in range(chips_plane):
                target = z * chips_plane + j
                both = mine1[target, k].astype(F32) + recv1[z, k, j].astype(F32)

                @pl.when(target == chip)
                def _():
                    sums[target, k] = both.astype(BF16)

                @pl.when(target != chip)
                def _():
                    mine1[target, k] = both.astype(BF16)
                    chip_copy(target, k).start()

        return carry

    lax.fori_loop(0, total + 1, step_body, 0)

    for k in range(chunks):

        def wait_sums(step, carry):
            source = (chip + step) % n_chip
            remote(
                mine1.at[source, k], sums.at[source, k], s2_ss.at[source, k], s2_rs.at[source, k],
                (2 * source + core, plane),
            ).wait_recv()
            return carry

        lax.fori_loop(1, n_chip, wait_sums, 0)
        acc = sums[0, k].astype(F32)
        for q in range(1, n_chip):
            acc += sums[q, k].astype(F32)
        out[k * width : (k + 1) * width, :] = acc.astype(BF16)

    def drain_blocks(step, carry):
        a_copy((me + step) % n_row).wait_send()
        return carry

    lax.fori_loop(1, n_row, drain_blocks, 0)

    def drain(n, carry):
        z, k = n // chunks, n % chunks
        core_copy(z, k).wait_send()

        @pl.when((z <= plane) & has_right)
        def _():
            to_right(z, k).wait_send()

        @pl.when((z >= plane) & has_left)
        def _():
            to_left(z, k).wait_send()

        for j in range(chips_plane):
            target = z * chips_plane + j

            @pl.when(target != chip)
            def _():
                chip_copy(target, k).wait_send()

        return carry

    lax.fori_loop(0, total, drain, 0)


def body(integrals, coeffs, mask, offsets, atom_of_slot):
    n_row = lax.axis_size("row")
    n_col = lax.axis_size("col")
    me = lax.axis_index("row")
    plane = lax.axis_index("col")
    per_dev, atom_w, row_width = integrals.shape
    rows, cols = coeffs.shape
    cap = max(2, -(-per_dev // n_row))
    slots = n_row * cap
    block = cols * n_col // n_row
    chunks = max(1, min(4, block // 128))
    width = block // chunks
    per_plane = n_row // n_col

    holders = atom_of_slot.reshape(n_row, per_dev)
    slot = jnp.arange(per_dev, dtype=jnp.int32)
    mine = lax.dynamic_slice_in_dim(atom_of_slot, me * per_dev, per_dev)
    owner = mine // per_dev
    before = (owner[None, :] == owner[:, None]) & (slot[None, :] < slot[:, None])
    position = owner * cap + jnp.sum(before.astype(jnp.int32), axis=1)
    order = jnp.sum(
        jnp.where(jnp.arange(slots, dtype=jnp.int32)[:, None] == position[None, :], slot[None, :], 0), axis=1
    )
    is_mine = holders // per_dev == me
    earlier = is_mine[:, None, :] & (slot[None, None, :] < slot[None, :, None])
    arrival = jnp.sum(earlier.astype(jnp.int32), axis=2)
    place = (jnp.arange(n_row, dtype=jnp.int32)[:, None] * cap + arrival).reshape(-1)
    pick = jnp.sum(
        jnp.where((me * per_dev + slot)[:, None] == atom_of_slot[None, :], place[None, :], 0), axis=1
    )
    bounds = lax.dynamic_slice_in_dim(offsets, me * per_dev, per_dev + 1)
    lengths = bounds[1:] - bounds[:-1]
    significant = lax.dynamic_slice(mask, (me * per_dev, plane), (per_dev, 1))[:, 0]
    meta = jnp.concatenate([order, pick, lengths, significant])

    packed = rows * 3 // 4
    dma = pltpu.SemaphoreType.DMA
    n_chip = n_row // 2
    pair_width = per_plane * width
    return pl.pallas_call(
        functools.partial(kernel, n_row, n_col, cap, chunks, width),
        out_shape=jax.ShapeDtypeStruct((block, row_width), BF16),
        in_specs=[pl.BlockSpec(memory_space=pltpu.SMEM)] + [pl.BlockSpec(memory_space=pltpu.VMEM)] * 2,
        out_specs=pl.BlockSpec(memory_space=pltpu.VMEM),
        scratch_shapes=[
            pltpu.VMEM((n_row, cap, atom_w, row_width), BF16),
            pltpu.VMEM((n_row, cap, atom_w, row_width), BF16),
            pltpu.VMEM((packed, row_width), BF16),
            pltpu.VMEM((n_col, chunks, packed, pair_width), BF16),
            pltpu.VMEM((n_chip, chunks, width, row_width), BF16),
            pltpu.VMEM((n_col, chunks, per_plane // 2, width, row_width), BF16),
            pltpu.VMEM((n_col, chunks, per_plane // 2, width, row_width), BF16),
            pltpu.VMEM((n_chip, chunks, width, row_width), BF16),
            dma((n_row,)),
            dma((n_row,)),
            dma((n_col, chunks)),
            dma((n_col, chunks)),
            dma((n_col, chunks)),
            dma((n_col, chunks)),
            dma((n_col, chunks)),
            dma((n_chip, chunks)),
            dma((n_chip, chunks)),
        ],
        compiler_params=pltpu.CompilerParams(
            collective_id=0, has_side_effects=True, vmem_limit_bytes=62 << 20
        ),
    )(meta, integrals, coeffs)


def solution(mesh):
    in_specs = (P("row", None, "col"), P("row", "col"), P(), P(), P())
    out_specs = P("row", "col")
    return jax.shard_map(body, mesh=mesh, in_specs=in_specs, out_specs=out_specs, check_vma=False)
```

time: 292 us -> 172 us (0.59); the launches traced: 289 us -> 172 us
  waiting for transfers between devices: 233 us -> 0 us
  Pallas kernels: 0 us -> 164 us
  matrix products: 22.8 us -> 0 us
  between operations: 13.5 us -> 0.04 us
  local copies, waits for them, and re-layouts: 13.7 us -> 3.35 us
  starting transfers between devices: 4.6 us -> 0 us
  other arithmetic: 1.58 us -> 5.12 us
    pallas_call x0 -> x1, Pallas kernels: none -> 164 us  [body(): pl.pallas_call(functools.partial(kernel, n_row, n_col, cap, chunks, width...]
    all_gather x1 -> x0, waiting for transfers between devices: 119 us -> none  [body(): coeff_piece = lax.all_gather(coeffs, 'col', axis=1, tiled=True)]
    reduce_scatter x1 -> x0, waiting for transfers between devices: 68.4 us -> none  [body(): lax.psum_scatter(partial_sums, 'row', scatter_dimension=0, tiled=True)]
    all_to_all x1 -> x0, waiting for transfers between devices: 44.2 us -> none  [body(): lax.all_to_all(outgoing, 'row', split_axis=0, concat_axis=0, tiled=True)]
    dot_general x3 -> x0, matrix products: 22.8 us -> none  [the longest x1 17.2 us: product(): lax.dot_general(coeff_piece, kept_rows, (((0,), (0,)), ((), ())), preferr...]
    reshape x2 -> x0, local copies, waits for them, and re-layouts: 7.26 us -> none  [the longest x1 3.88 us: body(): integrals.reshape(per_dev, atom_w * row_width)]
    all_to_all x1 -> x0, starting transfers between devices: 4.56 us -> none  [body(): lax.all_to_all(outgoing, 'row', split_axis=0, concat_axis=0, tiled=True)]
    mul x1 -> x0, local copies, waits for them, and re-layouts: 3.18 us -> none  [body(): blocks = ordered * keep_rows[:, :, None].astype(jnp.bfloat16)]
  transfers between devices with their start and end apart: 3 -> 0, of which waited for: 3 -> 0; matrix products, arithmetic and copies ran while one was open for 6% -> 0% of each run, Pallas kernels for 0% -> 0%
where the time goes in v1:
time: 172 us
  Pallas kernels  164 us (95%)
  other arithmetic  5.12 us (3%)
  local copies, waits for them, and re-layouts  3.35 us (2%)
    pallas_call x1, Pallas kernels, body(): pl.pallas_call(functools.partial(kernel, n_row, n_col, cap, chunks, width...  164 us

profile of v1, /device:TPU:7, one launch (start us, length us, event | category | flops | bytes accessed | tf_op | source)
XLA Modules:
  0.0 172.2 jit_solution(2187797398301164738)
XLA Ops:
  0.0 0.0 copy-start
  0.0 0.8 dynamic_slice.10
  0.8 0.1 slice_subtract_fusion
  0.8 0.0 copy-done
  0.8 0.1 dynamic-slice_bitcast_fusion
  0.9 0.8 and_select_fusion
  1.7 0.2 convert_reduce_fusion.1
  1.9 0.8 multiply_add_fusion
  2.6 0.1 select_reduce_fusion.1
  2.8 0.7 fusion.1
  3.5 0.1 and.36
  3.5 0.7 broadcast_divide_fusion
  4.2 0.1 div.21
  4.4 0.2 convert_reduce_fusion
  4.6 0.1 broadcast_add_fusion
  4.6 0.1 add.50
  4.7 0.9 select_reduce_fusion
  5.6 0.7 pad_add_fusion.meta
  6.2 163.7 %shard_map.55 = bf16[512,1024]{1,0:T(8,128)(2,1)} custom-call(s32[160]{0:T(256)} %pad_add_fusion.meta, bf16[40,32,1024]{2,1,0:T(8,128)(2,1)} %integrals.1, bf16[1280,1024]{1,0:T(8,128)(2,1)} %coeffs.1), custom_call_target="tpu_custom_call" | custom-call | tf_op jit(solution)/shard_map/pallas_call | solution.py:285
  169.9 2.3 %copy.7 = bf16[512,1024]{1,0:T(8,128)(2,1)} copy(bf16[512,1024]{1,0:T(8,128)(2,1)} %shard_map.55) | data formatting | bytes 2097152
  (4 shorter events, 0.0 us)
Async XLA Ops:
  0.0 0.8 copy-start

commit v2 on v1

--- a/solution.py
+++ b/solution.py
@@ -29,8 +29,8 @@
 def kernel(
     n_row, n_col, cap, chunks, width,
     meta, integrals, coeffs, out,
-    asend, arecv, kept, gathered, mine1, send1, recv1, sums,
-    a_ss, a_rs, r_ss, l_ss, g_rs, s1_ss, s1_rs, s2_ss, s2_rs,
+    asend, arecv, kept, gathered, mine1, send1, recv1, sums, kept_end, mine4, send4, recv4,
+    a_ss, a_rs, r_ss, l_ss, g_rs, s1_ss, s1_rs, s2_ss, s2_rs, k_ss, k_rs, s4_ss, s4_rs, s3_ss, s3_rs,
 ):
     me = lax.axis_index("row")
     plane = lax.axis_index("col")
@@ -50,6 +50,16 @@
     has_left = plane > 0
     has_right = plane < n_col - 1
 
+    share = n_col >= 4
+    pieces = chunks
+    piece = row_width // pieces
+    is_end = ((plane == 0) | (plane == n_col - 1)) & share
+    is_helper = ((plane == 1) | (plane == n_col - 2)) & share
+    low_half = plane <= n_col - 1 - plane
+    end_plane = jnp.where(low_half, 0, n_col - 1)
+    helper_plane = jnp.where(low_half, 1, n_col - 2)
+    mate_plane = jnp.where(is_end, helper_plane, end_plane)
+
     barrier = pltpu.get_barrier_semaphore()
     for other in range(1, n_row):
         pl.semaphore_signal(barrier, inc=1, device_id=((me + other) % n_row, plane), device_id_type=MESH)
@@ -61,6 +71,15 @@
     @pl.when(has_right)
     def _():
         pl.semaphore_signal(barrier, inc=1, device_id=(me, plane + 1), device_id_type=MESH)
+
+    @pl.when(is_end | is_helper)
+    def _():
+        def greet(step, carry):
+            mate = 2 * ((chip + step) % n_chip) + core
+            pl.semaphore_signal(barrier, inc=1, device_id=(mate, mate_plane), device_id_type=MESH)
+            return carry
+
+        lax.fori_loop(1, n_chip, greet, 0)
 
     def selection(p, weighted):
         s = lax.broadcasted_iota(jnp.int32, (packed, 2 * atom_w), 0)
@@ -86,7 +105,8 @@
         return carry
 
     lax.fori_loop(0, pairs, pack_coeffs, 0)
-    pl.semaphore_wait(barrier, n_row - 1 + has_left.astype(jnp.int32) + has_right.astype(jnp.int32))
+    extra_mates = jnp.where(is_end | is_helper, n_chip - 1, 0)
+    pl.semaphore_wait(barrier, n_row - 1 + has_left.astype(jnp.int32) + has_right.astype(jnp.int32) + extra_mates)
 
     def to_right(z, k):
         return remote(gathered.at[z, k], gathered.at[z, k], r_ss.at[z, k], g_rs.at[z, k], (me, plane + 1))
@@ -94,12 +114,20 @@
     def to_left(z, k):
         return remote(gathered.at[z, k], gathered.at[z, k], l_ss.at[z, k], g_rs.at[z, k], (me, plane - 1))
 
+    def goes_right(z):
+        ok = (z <= plane) & has_right
+        return ok & ((plane != n_col - 2) | (z == plane)) if share else ok
+
+    def goes_left(z):
+        ok = (z >= plane) & has_left
+        return ok & ((plane != 1) | (z == plane)) if share else ok
+
     def forward(z, k):
-        @pl.when((z <= plane) & has_right)
+        @pl.when(goes_right(z))
         def _():
             to_right(z, k).start()
 
-        @pl.when((z >= plane) & has_left)
+        @pl.when(goes_left(z))
         def _():
             to_left(z, k).start()
 
@@ -143,6 +171,21 @@
 
     lax.fori_loop(0, pairs, pack_kept, 0)
 
+    def piece_at(q):
+        return pl.ds(pl.multiple_of(q * piece, 128), piece)
+
+    def kept_copy(q):
+        return remote(
+            kept.at[:, piece_at(q)], kept_end.at[:, piece_at(q)], k_ss.at[q], k_rs.at[q], (me, helper_plane)
+        )
+
+    if share:
+
+        @pl.when(is_end)
+        def _():
+            for q in range(pieces):
+                kept_copy(q).start()
+
     def core_copy(z, k):
         return remote(send1.at[z, k], recv1.at[z, k], s1_ss.at[z, k], s1_rs.at[z, k], (partner, plane))
 
@@ -151,10 +194,81 @@
             mine1.at[target, k], sums.at[chip, k], s2_ss.at[target, k], s2_rs.at[chip, k], (2 * target + core, plane)
         )
 
-    total = n_col * chunks
+    steps = jnp.where(is_end, 2 * chunks, n_col * chunks)
+
+    def finish(n):
+        z = nearest(plane, n_col, n // chunks)
+        k = n % chunks
+        core_copy(z, k).wait_recv()
+        for j in range(chips_plane):
+            target = z * chips_plane + j
+            both = mine1[target, k].astype(F32) + recv1[z, k, j].astype(F32)
+
+            @pl.when(target == chip)
+            def _():
+                sums[target, k] = both.astype(BF16)
+
+            @pl.when(target != chip)
+            def _():
+                mine1[target, k] = both.astype(BF16)
+                chip_copy(target, k).start()
+
+    near = (n_col - 3) * chunks
+
+    def begin(t):
+        return near * t + t * t
+
+    def decode(e):
+        e = jnp.asarray(e, jnp.int32)
+        t = jnp.int32(0)
+        for w in range(1, chunks):
+            t += (e >= begin(w)).astype(jnp.int32)
+        u = e - begin(t)
+        last = u >= near
+        v = u - near
+        early = v <= t
+        far = jnp.where(last, n_col - 3, u // chunks)
+        k = jnp.where(last, jnp.where(early, v, t), u % chunks)
+        q = jnp.where(last & (v > t), v - 1 - t, t)
+        z = jnp.where(low_half, far + 2, n_col - 3 - far)
+        return far, z, k, q
+
+    def far_core_copy(far, k, q):
+        return remote(
+            send4.at[far, k, q], recv4.at[far, k, q], s4_ss.at[far, k, q], s4_rs.at[far, k, q], (partner, plane)
+        )
+
+    def far_copy(far, z, j, k, q):
+        target = z * chips_plane + j
+        return remote(
+            mine4.at[far, k, q, j], sums.at[chip, k, :, piece_at(q)], s3_ss.at[target, k, q], s3_rs.at[chip, k, q],
+            (2 * target + core, end_plane),
+        )
+
+    def far_start(e):
+        far, z, k, q = decode(e)
+
+        part = lax.dot_general(
+            gathered[z, k], kept_end[:, piece_at(q)], (((0,), (0,)), ((), ())), preferred_element_type=F32
+        ).astype(BF16)
+        for j in range(chips_plane):
+            lower = part[2 * j * width : (2 * j + 1) * width]
+            upper = part[(2 * j + 1) * width : (2 * j + 2) * width]
+            is_lower = core == 0
+            mine4[far, k, q, j] = jnp.where(is_lower, lower, upper)
+            send4[far, k, q, j] = jnp.where(is_lower, upper, lower)
+        far_core_copy(far, k, q).start()
+
+    def far_finish(e):
+        far, z, k, q = decode(e)
+        far_core_copy(far, k, q).wait_recv()
+        for j in range(chips_plane):
+            both = mine4[far, k, q, j].astype(F32) + recv4[far, k, q, j].astype(F32)
+            mine4[far, k, q, j] = both.astype(BF16)
+            far_copy(far, z, j, k, q).start()
 
     def step_body(n, carry):
-        @pl.when(n < total)
+        @pl.when(n < steps)
         def _():
             z = nearest(plane, n_col, n // chunks)
             k = n % chunks
@@ -177,37 +291,68 @@
 
         @pl.when(n > 0)
         def _():
-            z = nearest(plane, n_col, (n - 1) // chunks)
-            k = (n - 1) % chunks
-            core_copy(z, k).wait_recv()
-            for j in range(chips_plane):
-                target = z * chips_plane + j
-                both = mine1[target, k].astype(F32) + recv1[z, k, j].astype(F32)
-
-                @pl.when(target == chip)
-                def _():
-                    sums[target, k] = both.astype(BF16)
-
-                @pl.when(target != chip)
-                def _():
-                    mine1[target, k] = both.astype(BF16)
-                    chip_copy(target, k).start()
-
-        return carry
-
-    lax.fori_loop(0, total + 1, step_body, 0)
-
-    for k in range(chunks):
-
+            finish(n - 1)
+
+        if share:
+            t = n - (n_col - 1) * chunks
+
+            @pl.when(is_helper & (t >= 0) & (t < chunks))
+            def _():
+                kept_copy(t).wait_recv()
+
+                def far_body(e, carry):
+                    far_start(e)
+
+                    @pl.when(e > 0)
+                    def _():
+                        far_finish(e - 1)
+
+                    return carry
+
+                lax.fori_loop(begin(t), begin(t + 1), far_body, 0)
+
+        return carry
+
+    lax.fori_loop(0, steps + 1, step_body, 0)
+    if share:
+
+        @pl.when(is_helper)
+        def _():
+            far_finish(begin(chunks) - 1)
+
+    my_plane = chip // chips_plane
+    distance = jnp.where(low_half, my_plane, n_col - 1 - my_plane)
+    from_helper = is_end & (distance >= 2)
+
+    @pl.when(jnp.logical_not(from_helper))
+    def _():
         def wait_sums(step, carry):
             source = (chip + step) % n_chip
-            remote(
-                mine1.at[source, k], sums.at[source, k], s2_ss.at[source, k], s2_rs.at[source, k],
-                (2 * source + core, plane),
-            ).wait_recv()
+            for k in range(chunks):
+                remote(
+                    mine1.at[source, k], sums.at[source, k], s2_ss.at[source, k], s2_rs.at[source, k],
+                    (2 * source + core, plane),
+                ).wait_recv()
             return carry
 
         lax.fori_loop(1, n_chip, wait_sums, 0)
+
+    if share:
+
+        @pl.when(from_helper)
+        def _():
+            def wait_far(source, carry):
+                for k in range(chunks):
+                    for q in range(pieces):
+                        remote(
+                            mine4.at[0, k, q, 0], sums.at[source, k, :, piece_at(q)], s3_ss.at[source, k, q],
+                            s3_rs.at[source, k, q], (2 * source + core, helper_plane),
+                        ).wait_recv()
+                return carry
+
+            lax.fori_loop(0, n_chip, wait_far, 0)
+
+    for k in range(chunks):
         acc = sums[0, k].astype(F32)
         for q in range(1, n_chip):
             acc += sums[q, k].astype(F32)
@@ -220,14 +365,14 @@
     lax.fori_loop(1, n_row, drain_blocks, 0)
 
     def drain(n, carry):
-        z, k = n // chunks, n % chunks
+        z, k = nearest(plane, n_col, n // chunks), n % chunks
         core_copy(z, k).wait_send()
 
-        @pl.when((z <= plane) & has_right)
+        @pl.when(goes_right(z))
         def _():
             to_right(z, k).wait_send()
 
-        @pl.when((z >= plane) & has_left)
+        @pl.when(goes_left(z))
         def _():
             to_left(z, k).wait_send()
 
@@ -240,7 +385,24 @@
 
         return carry
 
-    lax.fori_loop(0, total, drain, 0)
+    lax.fori_loop(0, steps, drain, 0)
+    if share:
+
+        @pl.when(is_end)
+        def _():
+            for q in range(pieces):
+                kept_copy(q).wait_send()
+
+        @pl.when(is_helper)
+        def _():
+            def drain_far(e, carry):
+                far, z, k, q = decode(e)
+                far_core_copy(far, k, q).wait_send()
+                for j in range(chips_plane):
+                    far_copy(far, z, j, k, q).wait_send()
+                return carry
+
+            lax.fori_loop(0, begin(chunks), drain_far, 0)
 
 
 def body(integrals, coeffs, mask, offsets, atom_of_slot):
@@ -282,6 +444,8 @@
     dma = pltpu.SemaphoreType.DMA
     n_chip = n_row // 2
     pair_width = per_plane * width
+    n_far = max(1, n_col - 2)
+    far_shape = (n_far, chunks, chunks, per_plane // 2, width, row_width // chunks)
     return pl.pallas_call(
         functools.partial(kernel, n_row, n_col, cap, chunks, width),
         out_shape=jax.ShapeDtypeStruct((block, row_width), BF16),
@@ -296,6 +460,10 @@
             pltpu.VMEM((n_col, chunks, per_plane // 2, width, row_width), BF16),
             pltpu.VMEM((n_col, chunks, per_plane // 2, width, row_width), BF16),
             pltpu.VMEM((n_chip, chunks, width, row_width), BF16),
+            pltpu.VMEM((packed, row_width), BF16),
+            pltpu.VMEM(far_shape, BF16),
+            pltpu.VMEM(far_shape, BF16),
+            pltpu.VMEM(far_shape, BF16),
             dma((n_row,)),
             dma((n_row,)),
             dma((n_col, chunks)),
@@ -305,6 +473,12 @@
             dma((n_col, chunks)),
             dma((n_chip, chunks)),
             dma((n_chip, chunks)),
+            dma((chunks,)),
+            dma((chunks,)),
+            dma((n_far, chunks, chunks)),
+            dma((n_far, chunks, chunks)),
+            dma((n_chip, chunks, chunks)),
+            dma((n_chip, chunks, chunks)),
         ],
         compiler_params=pltpu.CompilerParams(
             collective_id=0, has_side_effects=True, vmem_limit_bytes=62 << 20

time: 172 us -> 148 us (0.86)
  Pallas kernels: 164 us -> 139 us
    pallas_call x1, Pallas kernels: 164 us -> 139 us  [body(): pl.pallas_call(functools.partial(kernel, n_row, n_col, cap, chunks, width...]
where the time goes in v2:
time: 148 us; the launch traced here: 147 us
  Pallas kernels  139 us (94%)
  other arithmetic  5.12 us (3%)
  local copies, waits for them, and re-layouts  3.35 us (2%)
    pallas_call x1, Pallas kernels, body(): pl.pallas_call(functools.partial(kernel, n_row, n_col, cap, chunks, width...  139 us

profile of v2, /device:TPU:7, one launch (start us, length us, event | category | flops | bytes accessed | tf_op | source)
XLA Modules:
  0.0 147.4 jit_solution(3692703934486611989)
XLA Ops:
  0.0 0.0 copy-start
  0.0 0.8 dynamic_slice.10
  0.8 0.1 slice_subtract_fusion
  0.8 0.0 copy-done
  0.8 0.1 dynamic-slice_bitcast_fusion
  0.9 0.8 and_select_fusion
  1.7 0.2 convert_reduce_fusion.1
  1.9 0.8 multiply_add_fusion
  2.6 0.1 select_reduce_fusion.1
  2.8 0.7 fusion.1
  3.5 0.1 and.36
  3.5 0.7 broadcast_divide_fusion
  4.2 0.1 div.21
  4.4 0.2 convert_reduce_fusion
  4.6 0.1 broadcast_add_fusion
  4.6 0.1 add.50
  4.7 0.9 select_reduce_fusion
  5.6 0.7 pad_add_fusion.meta
  6.2 138.9 %shard_map.55 = bf16[512,1024]{1,0:T(8,128)(2,1)} custom-call(s32[160]{0:T(256)} %pad_add_fusion.meta, bf16[40,32,1024]{2,1,0:T(8,128)(2,1)} %integrals.1, bf16[1280,1024]{1,0:T(8,128)(2,1)} %coeffs.1), custom_call_target="tpu_custom_call" | custom-call | tf_op jit(solution)/shard_map/pallas_call | solution.py:449
  145.2 2.3 %copy.7 = bf16[512,1024]{1,0:T(8,128)(2,1)} copy(bf16[512,1024]{1,0:T(8,128)(2,1)} %shard_map.55) | data formatting | bytes 2097152
  (4 shorter events, 0.0 us)
Async XLA Ops:
  0.0 0.8 copy-start

commit v3 on v2

--- a/solution.py
+++ b/solution.py
@@ -29,8 +29,8 @@
 def kernel(
     n_row, n_col, cap, chunks, width,
     meta, integrals, coeffs, out,
-    asend, arecv, kept, gathered, mine1, send1, recv1, sums, kept_end, mine4, send4, recv4,
-    a_ss, a_rs, r_ss, l_ss, g_rs, s1_ss, s1_rs, s2_ss, s2_rs, k_ss, k_rs, s4_ss, s4_rs, s3_ss, s3_rs,
+    asend, arecv, kept, gathered, mine1, send1, recv1, sums, kept_end, mine4, send4, recv4, relay,
+    a_ss, a_rs, r_ss, l_ss, g_rs, s1_ss, s1_rs, s2_ss, s2_rs, k_ss, k_rs, s4_ss, s4_rs, s3_ss, s3_rs, s5_ss, s5_rs,
 ):
     me = lax.axis_index("row")
     plane = lax.axis_index("col")
@@ -58,7 +58,6 @@
     low_half = plane <= n_col - 1 - plane
     end_plane = jnp.where(low_half, 0, n_col - 1)
     helper_plane = jnp.where(low_half, 1, n_col - 2)
-    mate_plane = jnp.where(is_end, helper_plane, end_plane)
 
     barrier = pltpu.get_barrier_semaphore()
     for other in range(1, n_row):
@@ -71,15 +70,6 @@
     @pl.when(has_right)
     def _():
         pl.semaphore_signal(barrier, inc=1, device_id=(me, plane + 1), device_id_type=MESH)
-
-    @pl.when(is_end | is_helper)
-    def _():
-        def greet(step, carry):
-            mate = 2 * ((chip + step) % n_chip) + core
-            pl.semaphore_signal(barrier, inc=1, device_id=(mate, mate_plane), device_id_type=MESH)
-            return carry
-
-        lax.fori_loop(1, n_chip, greet, 0)
 
     def selection(p, weighted):
         s = lax.broadcasted_iota(jnp.int32, (packed, 2 * atom_w), 0)
@@ -105,8 +95,7 @@
         return carry
 
     lax.fori_loop(0, pairs, pack_coeffs, 0)
-    extra_mates = jnp.where(is_end | is_helper, n_chip - 1, 0)
-    pl.semaphore_wait(barrier, n_row - 1 + has_left.astype(jnp.int32) + has_right.astype(jnp.int32) + extra_mates)
+    pl.semaphore_wait(barrier, n_row - 1 + has_left.astype(jnp.int32) + has_right.astype(jnp.int32))
 
     def to_right(z, k):
         return remote(gathered.at[z, k], gathered.at[z, k], r_ss.at[z, k], g_rs.at[z, k], (me, plane + 1))
@@ -238,11 +227,15 @@
             send4.at[far, k, q], recv4.at[far, k, q], s4_ss.at[far, k, q], s4_rs.at[far, k, q], (partner, plane)
         )
 
-    def far_copy(far, z, j, k, q):
-        target = z * chips_plane + j
+    def far_copy(far, k, q):
         return remote(
-            mine4.at[far, k, q, j], sums.at[chip, k, :, piece_at(q)], s3_ss.at[target, k, q], s3_rs.at[chip, k, q],
-            (2 * target + core, end_plane),
+            mine4.at[far, k, q], relay.at[far, k, q], s3_ss.at[far, k, q], s3_rs.at[far, k, q], (me, end_plane)
+        )
+
+    def relay_copy(far, j, k, q, target):
+        return remote(
+            relay.at[far, k, q, j], sums.at[chip, k, :, piece_at(q)], s5_ss.at[far, k, q, j], s5_rs.at[chip, k, q],
+            (2 * target + core, plane),
         )
 
     def far_start(e):
@@ -265,7 +258,7 @@
         for j in range(chips_plane):
             both = mine4[far, k, q, j].astype(F32) + recv4[far, k, q, j].astype(F32)
             mine4[far, k, q, j] = both.astype(BF16)
-            far_copy(far, z, j, k, q).start()
+        far_copy(far, k, q).start()
 
     def step_body(n, carry):
         @pl.when(n < steps)
@@ -320,6 +313,26 @@
         def _():
             far_finish(begin(chunks) - 1)
 
+        @pl.when(is_end)
+        def _():
+            def pass_on(e, carry):
+                far, z, k, q = decode(e)
+                far_copy(far, k, q).wait_recv()
+                for j in range(chips_plane):
+                    target = z * chips_plane + j
+
+                    @pl.when(target == chip)
+                    def _():
+                        sums[target, k, :, piece_at(q)] = relay[far, k, q, j]
+
+                    @pl.when(target != chip)
+                    def _():
+                        relay_copy(far, j, k, q, target).start()
+
+                return carry
+
+            lax.fori_loop(0, begin(chunks), pass_on, 0)
+
     my_plane = chip // chips_plane
     distance = jnp.where(low_half, my_plane, n_col - 1 - my_plane)
     from_helper = is_end & (distance >= 2)
@@ -341,16 +354,17 @@
 
         @pl.when(from_helper)
         def _():
-            def wait_far(source, carry):
+            def wait_far(step, carry):
+                source = (chip + step) % n_chip
                 for k in range(chunks):
                     for q in range(pieces):
                         remote(
-                            mine4.at[0, k, q, 0], sums.at[source, k, :, piece_at(q)], s3_ss.at[source, k, q],
-                            s3_rs.at[source, k, q], (2 * source + core, helper_plane),
+                            relay.at[0, k, q, 0], sums.at[source, k, :, piece_at(q)], s5_ss.at[0, k, q, 0],
+                            s5_rs.at[source, k, q], (2 * source + core, plane),
                         ).wait_recv()
                 return carry
 
-            lax.fori_loop(0, n_chip, wait_far, 0)
+            lax.fori_loop(1, n_chip, wait_far, 0)
 
     for k in range(chunks):
         acc = sums[0, k].astype(F32)
@@ -393,13 +407,25 @@
             for q in range(pieces):
                 kept_copy(q).wait_send()
 
+            def drain_relay(e, carry):
+                far, z, k, q = decode(e)
+                for j in range(chips_plane):
+                    target = z * chips_plane + j
+
+                    @pl.when(target != chip)
+                    def _():
+                        relay_copy(far, j, k, q, target).wait_send()
+
+                return carry
+
+            lax.fori_loop(0, begin(chunks), drain_relay, 0)
+
         @pl.when(is_helper)
         def _():
             def drain_far(e, carry):
                 far, z, k, q = decode(e)
                 far_core_copy(far, k, q).wait_send()
-                for j in range(chips_plane):
-                    far_copy(far, z, j, k, q).wait_send()
+                far_copy(far, k, q).wait_send()
                 return carry
 
             lax.fori_loop(0, begin(chunks), drain_far, 0)
@@ -464,6 +490,7 @@
             pltpu.VMEM(far_shape, BF16),
             pltpu.VMEM(far_shape, BF16),
             pltpu.VMEM(far_shape, BF16),
+            pltpu.VMEM(far_shape, BF16),
             dma((n_row,)),
             dma((n_row,)),
             dma((n_col, chunks)),
@@ -477,7 +504,9 @@
             dma((chunks,)),
             dma((n_far, chunks, chunks)),
             dma((n_far, chunks, chunks)),
-            dma((n_chip, chunks, chunks)),
+            dma((n_far, chunks, chunks)),
+            dma((n_far, chunks, chunks)),
+            dma((n_far, chunks, chunks, per_plane // 2)),
             dma((n_chip, chunks, chunks)),
         ],
         compiler_params=pltpu.CompilerParams(

time: 148 us -> 148 us (level)
  no operation moved by 1% of the time
where the time goes in v3:
time: 148 us; the launch traced here: 147 us
  Pallas kernels  139 us (94%)
  other arithmetic  5.12 us (3%)
  local copies, waits for them, and re-layouts  3.35 us (2%)
    pallas_call x1, Pallas kernels, body(): pl.pallas_call(functools.partial(kernel, n_row, n_col, cap, chunks, width...  139 us

profile of v3, /device:TPU:7, one launch (start us, length us, event | category | flops | bytes accessed | tf_op | source)
XLA Modules:
  0.0 147.3 jit_solution(1838857558494728377)
XLA Ops:
  0.0 0.0 copy-start
  0.0 0.8 dynamic_slice.10
  0.8 0.1 slice_subtract_fusion
  0.8 0.0 copy-done
  0.8 0.1 dynamic-slice_bitcast_fusion
  0.9 0.8 and_select_fusion
  1.7 0.2 convert_reduce_fusion.1
  1.9 0.8 multiply_add_fusion
  2.6 0.1 select_reduce_fusion.1
  2.8 0.7 fusion.1
  3.5 0.1 and.36
  3.5 0.7 broadcast_divide_fusion
  4.2 0.1 div.21
  4.4 0.2 convert_reduce_fusion
  4.6 0.1 broadcast_add_fusion
  4.6 0.1 add.50
  4.7 0.9 select_reduce_fusion
  5.6 0.7 pad_add_fusion.meta
  6.2 138.8 %shard_map.55 = bf16[512,1024]{1,0:T(8,128)(2,1)} custom-call(s32[160]{0:T(256)} %pad_add_fusion.meta, bf16[40,32,1024]{2,1,0:T(8,128)(2,1)} %integrals.1, bf16[1280,1024]{1,0:T(8,128)(2,1)} %coeffs.1), custom_call_target="tpu_custom_call" | custom-call | tf_op jit(solution)/shard_map/pallas_call | solution.py:475
  145.0 2.3 %copy.7 = bf16[512,1024]{1,0:T(8,128)(2,1)} copy(bf16[512,1024]{1,0:T(8,128)(2,1)} %shard_map.55) | data formatting | bytes 2097152
  (4 shorter events, 0.0 us)
Async XLA Ops:
  0.0 0.8 copy-start
